TPU v7x, 32 devices: a whole 2x2x4 slice. The times are simulated.
32 devices in a mesh: gx: 4 (over y, core), gy: 8 (over z, x).
Axes of the slice: x: 2, y: 2, z: 4, core: 2. Of those that a mesh axis runs over, the one named last changes fastest.
Arguments:
- source: float32 [64, 16, 1024], P(None, 'gx', 'gy'), may hold values from -6 to 6
- initial: float32 [64, 16, 1024], P(None, 'gx', 'gy'), may hold values from -6 to 6
- reaction: float32 [64, 16, 1024], P(None, 'gx', 'gy'), may hold values from 1 to 3
- stiffness: float32 [16, 1024], P('gx', 'gy'), may hold values from 0.5 to 2
- line_op: float32 [8, 8], replicated, may hold values from -1.6 to 5.6
- face_deriv: float32 [8], replicated, may hold values from -2 to 2
- wall_flags: int32 [4, 16, 1024], P(None, 'gx', 'gy'), may hold values 0 or 1
Outputs:
- hessenberg: float32 [6, 5], replicated
- krylov_basis: float32 [6, 64, 16, 1024], P(None, None, 'gx', 'gy')
All inputs are finite; a program needn't handle non-finite values. No bound on the sum of `wall_flags` on one device may be relied on, other than what follows from the above.
Results may differ from a plain program's by a relative error of at most 0.0003.
Values sent between devices are 32-bit elements; how exact they have to be, the bound alone decides.
A program may use at most 64 MiB of HBM per device.

v0:
```python
import jax
import jax.numpy as jnp
from jax import lax
from jax.sharding import PartitionSpec as P

P_SIZE = 8
ITERS = 5
TAU = 2.0
FLOOR = 0.1


def extended(array, sides, width):
    for axis, dim in sides:
        devices, length = (lax.axis_size(axis), array.shape[dim])
        up = [(i, (i + 1) % devices) for i in range(devices)]
        down = [(j, i) for i, j in up]
        last = lax.slice_in_dim(array, length - width, length, axis=dim)
        leading = lax.slice_in_dim(array, 0, width, axis=dim)
        before = lax.ppermute(last, axis, up)
        after = lax.ppermute(leading, axis, down)
        array = jnp.concatenate([before, array, after], axis=dim)
    return array


def local_total(values):
    return jnp.sum(jnp.sum(values, axis=0))


def x_traces(nodes, face_deriv):
    highest = lax.Precision.HIGHEST
    lower = jnp.einsum("c,cbxy->bxy", face_deriv, nodes, precision=highest)
    upper = jnp.einsum("c,cbxy->bxy", face_deriv[::-1], nodes, precision=highest)
    return jnp.stack([nodes[0], lower, nodes[-1], upper])


def y_traces(nodes, face_deriv):
    highest = lax.Precision.HIGHEST
    lower = jnp.einsum("c,acxy->axy", face_deriv, nodes, precision=highest)
    upper = jnp.einsum("c,acxy->axy", face_deriv[::-1], nodes, precision=highest)
    return jnp.stack([nodes[:, 0], lower, nodes[:, -1], upper])


def apply_op(field, reaction, stiffness, line_op, face_deriv, opened):
    highest = lax.Precision.HIGHEST
    nodes = field.reshape(P_SIZE, P_SIZE, field.shape[1], field.shape[2])
    interior = stiffness * (
        jnp.einsum("ac,cbxy->abxy", line_op, nodes, precision=highest)
        + jnp.einsum("bc,acxy->abxy", line_op, nodes, precision=highest)
    )
    padded = extended(nodes, (("gx", 2), ("gy", 3)), 1)
    xside = x_traces(padded, face_deriv)[:, :, :, 1:-1]
    yside = y_traces(padded, face_deriv)[:, :, 1:-1, :]
    x_own = xside[:, :, 1:-1]
    y_own = yside[:, :, :, 1:-1]
    east_nb = xside[0:2, :, 2:]
    west_nb = xside[2:4, :, :-2]
    north_nb = yside[0:2, :, :, 2:]
    south_nb = yside[2:4, :, :, :-2]
    add_east = TAU * (x_own[2] - opened[1] * east_nb[0]) + 0.5 * (x_own[3] - opened[1] * east_nb[1])
    add_west = TAU * (x_own[0] - opened[0] * west_nb[0]) + 0.5 * (x_own[1] - opened[0] * west_nb[1])
    add_north = TAU * (y_own[2] - opened[3] * north_nb[0]) + 0.5 * (
        y_own[3] - opened[3] * north_nb[1]
    )
    add_south = TAU * (y_own[0] - opened[2] * south_nb[0]) + 0.5 * (
        y_own[1] - opened[2] * south_nb[1]
    )
    result = reaction.reshape(nodes.shape) * nodes + interior
    result = result.at[0].add(add_west).at[P_SIZE - 1].add(add_east)
    result = result.at[:, 0].add(add_south).at[:, P_SIZE - 1].add(add_north)
    return result.reshape(field.shape)


def norm_scale(vector, total):
    squares = lax.psum(local_total(vector * vector), ("gx", "gy"))
    return jnp.sqrt(squares / total + FLOOR)


def body(source, initial, reaction, stiffness, line_op, face_deriv, wall_flags):
    highest = lax.Precision.HIGHEST
    total = float(
        P_SIZE
        * P_SIZE
        * source.shape[1]
        * lax.axis_size("gx")
        * source.shape[2]
        * lax.axis_size("gy")
    )
    opened = 1.0 - wall_flags.astype(jnp.float32)

    def operate(field):
        return apply_op(field, reaction, stiffness, line_op, face_deriv, opened)

    def products(basis, image):
        per_cell = jnp.einsum("kqxy,qxy->kxy", basis, image, precision=highest)
        return jnp.sum(per_cell, axis=(1, 2))

    first = source - operate(initial)
    basis = jnp.zeros((ITERS + 1,) + source.shape, jnp.float32)
    hessen = jnp.zeros((ITERS + 1, ITERS), jnp.float32)
    rows = lax.broadcasted_iota(jnp.int32, (ITERS + 1, ITERS), 0)
    cols = lax.broadcasted_iota(jnp.int32, (ITERS + 1, ITERS), 1)
    slots = lax.broadcasted_iota(jnp.int32, (ITERS + 1,), 0)

    def advance(step, carry):
        basis, hessen, pending = carry
        image = operate(pending)
        local = products(basis, image)
        projected, crossed, squares = lax.psum(
            (local, local_total(pending * image), local_total(pending * pending)), ("gx", "gy")
        )
        beta = jnp.sqrt(squares / total + FLOOR)
        basis = lax.dynamic_update_index_in_dim(basis, pending / beta, step, 0)
        coeffs = projected / (total * beta) + jnp.where(
            slots == step, crossed / (total * beta * beta), 0.0
        )
        pending = image / beta - jnp.einsum("k,kqxy->qxy", coeffs, basis, precision=highest)
        hessen = hessen + jnp.where(cols == step, coeffs[:, None], 0.0)
        hessen = hessen + jnp.where((rows == step) & (cols == step - 1), beta, 0.0)
        return (basis, hessen, pending)

    basis, hessen, pending = lax.fori_loop(0, ITERS, advance, (basis, hessen, first))
    beta = norm_scale(pending, total)
    basis = basis.at[ITERS].set(pending / beta)
    hessen = hessen + jnp.where((rows == ITERS) & (cols == ITERS - 1), beta, 0.0)
    return (hessen, basis)


def solution(mesh):
    return jax.shard_map(
        body,
        mesh=mesh,
        in_specs=(
            P(None, "gx", "gy"),
            P(None, "gx", "gy"),
            P(None, "gx", "gy"),
            P("gx", "gy"),
            P(),
            P(),
            P(None, "gx", "gy"),
        ),
        out_specs=(P(), P(None, None, "gx", "gy")),
        check_vma=False,
    )
```

profile of v0, /device:TPU:0, one launch (start us, length us, event | category | flops | bytes accessed | tf_op | source)
XLA Modules:
  0.0 408.1 jit_solution(16767970016116543631)
XLA Ops:
  2.2 2.0 collective-permute-start.5
  6.0 2.2 collective-permute-start.6
  8.2 3.1 collective-permute-start.7
  12.3 4.8 %collective-permute-done.6 = f32[8,8,6,1]{3,0,2,1:T(8,128)S(1)} collective-permute-done((f32[8,8,6,1]{3,0,2,1:T(8,128)S(1)}, f32[8,8,6,1]{3,0,2,1:T(8,128)S(1)}, u32[]{:S(2)}, u32[]{:S(2)}) %collective-permute-start.6) | collective-permute-done | bytes 1568 | tf_op jit(solution)/shard_map/ppermute | solution.py:19
  17.1 2.8 collective-permute-done.7
  26.0 339.5 %while.31 = (s32[]{:T(128)}, f32[6,64,4,128]{3,2,1,0:T(4,128)S(1)}, f32[6,5]{1,0:T(8,128)S(1)}, f32[64,4,128]{2,1,0:T(4,128)S(1)}, f32[64,4,128]{2,0,1:T(8,128)S...) while((s32[]{:T(128)}, f32[6,64,4,128]{3,2,1,0:T(4,128)S(1)}, ...), condition=%wide.region_6.7_spmd.clone.clone, body=%wide.region_0.6_spmd.clone.clone.sunk | while | flops 14006069 | bytes 9489035 | solution.py:121
  29.6 2.8 collective-permute-start.2
  32.7 4.3 %collective-permute-done.2 = f32[8,8,6,1]{3,0,2,1:T(8,128)S(1)} collective-permute-done((f32[8,8,6,1]{3,0,2,1:T(8,128)S(1)}, f32[8,8,6,1]{3,0,2,1:T(8,128)S(1)}, u32[]{:S(2)}, u32[]{:S(2)}) %collective-permute-start.2) | collective-permute-done | bytes 1568 | tf_op jit(solution)/shard_map/while/body/eval_jaxpr/ppermute | solution.py:20
  37.0 5.2 %collective-permute-done.3 = f32[8,8,6,1]{3,0,2,1:T(8,128)S(1)} collective-permute-done((f32[8,8,6,1]{3,0,2,1:T(8,128)S(1)}, f32[8,8,6,1]{3,0,2,1:T(8,128)S(1)}, u32[]{:S(2)}, u32[]{:S(2)}) %collective-permute-start.3) | collective-permute-done | bytes 1568 | tf_op jit(solution)/shard_map/while/body/eval_jaxpr/ppermute | solution.py:19
  47.3 2.6 convolution_bitcast_fusion.2
  49.8 39.4 %all-reduce.2 = (f32[]{:T(128)}, f32[6]{0:T(128)S(1)}, f32[]{:T(128)}) all-reduce(f32[]{:T(128)} %get-tuple-element.835, f32[6]{0:T(128)S(1)} %convolution_bitcast_fusion.2, f32[]{:T(128)} %fusion.189), channel_id=1, replica_groups=mesh['gx'=4,'gy'=8] {'gx','gy'}, use_global_device_ids=true, to_apply=%region_2.2 | all-reduce | flops 8 | bytes 64 | tf_op jit(solution)/shard_map/while/body/eval_jaxpr/psum | solution.py:108
  96.8 3.9 collective-permute-start.2
  101.0 4.9 %collective-permute-done.2 = f32[8,8,6,1]{3,0,2,1:T(8,128)S(1)} collective-permute-done((f32[8,8,6,1]{3,0,2,1:T(8,128)S(1)}, f32[8,8,6,1]{3,0,2,1:T(8,128)S(1)}, u32[]{:S(2)}, u32[]{:S(2)}) %collective-permute-start.2) | collective-permute-done | bytes 1568 | tf_op jit(solution)/shard_map/while/body/eval_jaxpr/ppermute | solution.py:20
  105.9 5.1 %collective-permute-done.3 = f32[8,8,6,1]{3,0,2,1:T(8,128)S(1)} collective-permute-done((f32[8,8,6,1]{3,0,2,1:T(8,128)S(1)}, f32[8,8,6,1]{3,0,2,1:T(8,128)S(1)}, u32[]{:S(2)}, u32[]{:S(2)}) %collective-permute-start.3) | collective-permute-done | bytes 1568 | tf_op jit(solution)/shard_map/while/body/eval_jaxpr/ppermute | solution.py:19
  116.0 2.6 convolution_bitcast_fusion.2
  118.6 39.2 %all-reduce.2 = (f32[]{:T(128)}, f32[6]{0:T(128)S(1)}, f32[]{:T(128)}) all-reduce(f32[]{:T(128)} %get-tuple-element.835, f32[6]{0:T(128)S(1)} %convolution_bitcast_fusion.2, f32[]{:T(128)} %fusion.189), channel_id=1, replica_groups=mesh['gx'=4,'gy'=8] {'gx','gy'}, use_global_device_ids=true, to_apply=%region_2.2 | all-reduce | flops 8 | bytes 64 | tf_op jit(solution)/shard_map/while/body/eval_jaxpr/psum | solution.py:108
  165.4 3.9 collective-permute-start.2
  169.6 4.6 %collective-permute-done.2 = f32[8,8,6,1]{3,0,2,1:T(8,128)S(1)} collective-permute-done((f32[8,8,6,1]{3,0,2,1:T(8,128)S(1)}, f32[8,8,6,1]{3,0,2,1:T(8,128)S(1)}, u32[]{:S(2)}, u32[]{:S(2)}) %collective-permute-start.2) | collective-permute-done | bytes 1568 | tf_op jit(solution)/shard_map/while/body/eval_jaxpr/ppermute | solution.py:20
  174.2 4.9 %collective-permute-done.3 = f32[8,8,6,1]{3,0,2,1:T(8,128)S(1)} collective-permute-done((f32[8,8,6,1]{3,0,2,1:T(8,128)S(1)}, f32[8,8,6,1]{3,0,2,1:T(8,128)S(1)}, u32[]{:S(2)}, u32[]{:S(2)}) %collective-permute-start.3) | collective-permute-done | bytes 1568 | tf_op jit(solution)/shard_map/while/body/eval_jaxpr/ppermute | solution.py:19
  184.1 2.6 convolution_bitcast_fusion.2
  186.7 39.1 %all-reduce.2 = (f32[]{:T(128)}, f32[6]{0:T(128)S(1)}, f32[]{:T(128)}) all-reduce(f32[]{:T(128)} %get-tuple-element.835, f32[6]{0:T(128)S(1)} %convolution_bitcast_fusion.2, f32[]{:T(128)} %fusion.189), channel_id=1, replica_groups=mesh['gx'=4,'gy'=8] {'gx','gy'}, use_global_device_ids=true, to_apply=%region_2.2 | all-reduce | flops 8 | bytes 64 | tf_op jit(solution)/shard_map/while/body/eval_jaxpr/psum | solution.py:108
  233.3 3.9 collective-permute-start.2
  237.6 4.6 %collective-permute-done.2 = f32[8,8,6,1]{3,0,2,1:T(8,128)S(1)} collective-permute-done((f32[8,8,6,1]{3,0,2,1:T(8,128)S(1)}, f32[8,8,6,1]{3,0,2,1:T(8,128)S(1)}, u32[]{:S(2)}, u32[]{:S(2)}) %collective-permute-start.2) | collective-permute-done | bytes 1568 | tf_op jit(solution)/shard_map/while/body/eval_jaxpr/ppermute | solution.py:20
  242.1 4.9 %collective-permute-done.3 = f32[8,8,6,1]{3,0,2,1:T(8,128)S(1)} collective-permute-done((f32[8,8,6,1]{3,0,2,1:T(8,128)S(1)}, f32[8,8,6,1]{3,0,2,1:T(8,128)S(1)}, u32[]{:S(2)}, u32[]{:S(2)}) %collective-permute-start.3) | collective-permute-done | bytes 1568 | tf_op jit(solution)/shard_map/while/body/eval_jaxpr/ppermute | solution.py:19
  252.1 2.6 convolution_bitcast_fusion.2
  254.7 39.1 %all-reduce.2 = (f32[]{:T(128)}, f32[6]{0:T(128)S(1)}, f32[]{:T(128)}) all-reduce(f32[]{:T(128)} %get-tuple-element.835, f32[6]{0:T(128)S(1)} %convolution_bitcast_fusion.2, f32[]{:T(128)} %fusion.189), channel_id=1, replica_groups=mesh['gx'=4,'gy'=8] {'gx','gy'}, use_global_device_ids=true, to_apply=%region_2.2 | all-reduce | flops 8 | bytes 64 | tf_op jit(solution)/shard_map/while/body/eval_jaxpr/psum | solution.py:108
  301.3 3.9 collective-permute-start.2
  305.5 4.6 %collective-permute-done.2 = f32[8,8,6,1]{3,0,2,1:T(8,128)S(1)} collective-permute-done((f32[8,8,6,1]{3,0,2,1:T(8,128)S(1)}, f32[8,8,6,1]{3,0,2,1:T(8,128)S(1)}, u32[]{:S(2)}, u32[]{:S(2)}) %collective-permute-start.2) | collective-permute-done | bytes 1568 | tf_op jit(solution)/shard_map/while/body/eval_jaxpr/ppermute | solution.py:20
  310.1 4.9 %collective-permute-done.3 = f32[8,8,6,1]{3,0,2,1:T(8,128)S(1)} collective-permute-done((f32[8,8,6,1]{3,0,2,1:T(8,128)S(1)}, f32[8,8,6,1]{3,0,2,1:T(8,128)S(1)}, u32[]{:S(2)}, u32[]{:S(2)}) %collective-permute-start.3) | collective-permute-done | bytes 1568 | tf_op jit(solution)/shard_map/while/body/eval_jaxpr/ppermute | solution.py:19
  320.0 2.6 convolution_bitcast_fusion.2
  322.6 39.1 %all-reduce.2 = (f32[]{:T(128)}, f32[6]{0:T(128)S(1)}, f32[]{:T(128)}) all-reduce(f32[]{:T(128)} %get-tuple-element.835, f32[6]{0:T(128)S(1)} %convolution_bitcast_fusion.2, f32[]{:T(128)} %fusion.189), channel_id=1, replica_groups=mesh['gx'=4,'gy'=8] {'gx','gy'}, use_global_device_ids=true, to_apply=%region_2.2 | all-reduce | flops 8 | bytes 64 | tf_op jit(solution)/shard_map/while/body/eval_jaxpr/psum | solution.py:108
  366.2 40.3 %psum.52 = f32[]{:T(128)} all-reduce(f32[]{:T(128)} %multiply_reduce_fusion.2), channel_id=1, replica_groups=mesh['gx'=4,'gy'=8] {'gx','gy'}, use_global_device_ids=true, to_apply=%region_8.9 | all-reduce | flops 1 | bytes 8 | tf_op jit(solution)/shard_map/psum | solution.py:74
  (322 shorter events, 68.2 us)
Async XLA Ops:
  1.5 2.6 copy-start.5
  1.6 4.1 %collective-permute-start.4 = (f32[8,8,1,128]{3,0,2,1:T(8,128)S(1)}, f32[8,8,1,128]{3,0,2,1:T(8,128)S(1)}, u32[]{:S(2)}, u32[]{:S(2)}) collective-permute-start(f32[8,8,1,128]{3,0,2,1:T(8,128)S(1)} %copy.247), channel_id=1, source_target_pairs={{0,8},{8,16},{16,24},{24,0},{1,9},{9,17},{17,25},{25,1},{2,10},{10... | collective-permute-start | bytes 98312 | tf_op jit(solution)/shard_map/ppermute | solution.py:19
  2.1 2.1 copy-start.11
  2.2 3.7 collective-permute-start.5
  5.5 6.7 %copy-start.3 = (f32[8,8,4,128]{3,0,2,1:T(8,128)}, f32[8,8,4,128]{3,0,2,1:T(8,128)S(1)}, u32[]{:S(2)}) copy-start(f32[8,8,4,128]{3,0,2,1:T(8,128)S(1)} %fusion.62) | copy-start | bytes 393220
  6.0 11.1 %collective-permute-start.6 = (f32[8,8,6,1]{3,0,2,1:T(8,128)S(1)}, f32[8,8,6,1]{3,0,2,1:T(8,128)S(1)}, u32[]{:S(2)}, u32[]{:S(2)}) collective-permute-start(f32[8,8,6,1]{3,0,2,1:T(8,128)S(1)} %get-tuple-element.682), channel_id=1, source_target_pairs={{0,1},{1,2},{2,3},{3,4},{4,5},{5,6},{6,7},{7,0},{8,9},{9,10},{10,1... | collective-permute-start | bytes 4616 | tf_op jit(solution)/shard_map/ppermute | solution.py:19
  8.2 11.6 %collective-permute-start.7 = (f32[8,8,6,1]{3,0,2,1:T(8,128)S(1)}, f32[8,8,6,1]{3,0,2,1:T(8,128)S(1)}, u32[]{:S(2)}, u32[]{:S(2)}) collective-permute-start(f32[8,8,6,1]{3,0,2,1:T(8,128)S(1)} %get-tuple-element.683), channel_id=1, source_target_pairs={{1,0},{2,1},{3,2},{4,3},{5,4},{6,5},{7,6},{0,7},{9,8},{10,9},{11,1... | collective-permute-start | bytes 4616 | tf_op jit(solution)/shard_map/ppermute | solution.py:20
  26.1 3.4 collective-permute-start
  26.3 3.2 collective-permute-start.1
  28.5 4.2 %copy-start.1 = (f32[8,8,4,128]{3,0,2,1:T(8,128)}, f32[8,8,4,128]{3,0,2,1:T(8,128)S(1)}, u32[]{:S(2)}) copy-start(f32[8,8,4,128]{3,0,2,1:T(8,128)S(1)} %fusion.175) | copy-start | bytes 393220 | tf_op jit(solution)/shard_map/while
  29.6 7.4 %collective-permute-start.2 = (f32[8,8,6,1]{3,0,2,1:T(8,128)S(1)}, f32[8,8,6,1]{3,0,2,1:T(8,128)S(1)}, u32[]{:S(2)}, u32[]{:S(2)}) collective-permute-start(f32[8,8,6,1]{3,0,2,1:T(8,128)S(1)} %get-tuple-element.788), channel_id=1, source_target_pairs={{1,0},{2,1},{3,2},{4,3},{5,4},{6,5},{7,6},{0,7},{9,8},{10,9},{11,1... | collective-permute-start | bytes 4616 | tf_op jit(solution)/shard_map/while/body/eval_jaxpr/ppermute | solution.py:20
  32.4 9.8 %collective-permute-start.3 = (f32[8,8,6,1]{3,0,2,1:T(8,128)S(1)}, f32[8,8,6,1]{3,0,2,1:T(8,128)S(1)}, u32[]{:S(2)}, u32[]{:S(2)}) collective-permute-start(f32[8,8,6,1]{3,0,2,1:T(8,128)S(1)} %get-tuple-element.789), channel_id=1, source_target_pairs={{0,1},{1,2},{2,3},{3,4},{4,5},{5,6},{6,7},{7,0},{8,9},{9,10},{10,1... | collective-permute-start | bytes 4616 | tf_op jit(solution)/shard_map/while/body/eval_jaxpr/ppermute | solution.py:19
  93.1 3.4 collective-permute-start
  93.2 3.5 collective-permute-start.1
  95.5 5.4 %copy-start.1 = (f32[8,8,4,128]{3,0,2,1:T(8,128)}, f32[8,8,4,128]{3,0,2,1:T(8,128)S(1)}, u32[]{:S(2)}) copy-start(f32[8,8,4,128]{3,0,2,1:T(8,128)S(1)} %fusion.175) | copy-start | bytes 393220 | tf_op jit(solution)/shard_map/while
  96.8 9.2 %collective-permute-start.2 = (f32[8,8,6,1]{3,0,2,1:T(8,128)S(1)}, f32[8,8,6,1]{3,0,2,1:T(8,128)S(1)}, u32[]{:S(2)}, u32[]{:S(2)}) collective-permute-start(f32[8,8,6,1]{3,0,2,1:T(8,128)S(1)} %get-tuple-element.788), channel_id=1, source_target_pairs={{1,0},{2,1},{3,2},{4,3},{5,4},{6,5},{7,6},{0,7},{9,8},{10,9},{11,1... | collective-permute-start | bytes 4616 | tf_op jit(solution)/shard_map/while/body/eval_jaxpr/ppermute | solution.py:20
  100.7 10.3 %collective-permute-start.3 = (f32[8,8,6,1]{3,0,2,1:T(8,128)S(1)}, f32[8,8,6,1]{3,0,2,1:T(8,128)S(1)}, u32[]{:S(2)}, u32[]{:S(2)}) collective-permute-start(f32[8,8,6,1]{3,0,2,1:T(8,128)S(1)} %get-tuple-element.789), channel_id=1, source_target_pairs={{0,1},{1,2},{2,3},{3,4},{4,5},{5,6},{6,7},{7,0},{8,9},{9,10},{10,1... | collective-permute-start | bytes 4616 | tf_op jit(solution)/shard_map/while/body/eval_jaxpr/ppermute | solution.py:19
  161.7 3.4 collective-permute-start
  161.8 3.5 collective-permute-start.1
  164.1 5.4 %copy-start.1 = (f32[8,8,4,128]{3,0,2,1:T(8,128)}, f32[8,8,4,128]{3,0,2,1:T(8,128)S(1)}, u32[]{:S(2)}) copy-start(f32[8,8,4,128]{3,0,2,1:T(8,128)S(1)} %fusion.175) | copy-start | bytes 393220 | tf_op jit(solution)/shard_map/while
  165.4 8.8 %collective-permute-start.2 = (f32[8,8,6,1]{3,0,2,1:T(8,128)S(1)}, f32[8,8,6,1]{3,0,2,1:T(8,128)S(1)}, u32[]{:S(2)}, u32[]{:S(2)}) collective-permute-start(f32[8,8,6,1]{3,0,2,1:T(8,128)S(1)} %get-tuple-element.788), channel_id=1, source_target_pairs={{1,0},{2,1},{3,2},{4,3},{5,4},{6,5},{7,6},{0,7},{9,8},{10,9},{11,1... | collective-permute-start | bytes 4616 | tf_op jit(solution)/shard_map/while/body/eval_jaxpr/ppermute | solution.py:20
  169.3 9.8 %collective-permute-start.3 = (f32[8,8,6,1]{3,0,2,1:T(8,128)S(1)}, f32[8,8,6,1]{3,0,2,1:T(8,128)S(1)}, u32[]{:S(2)}, u32[]{:S(2)}) collective-permute-start(f32[8,8,6,1]{3,0,2,1:T(8,128)S(1)} %get-tuple-element.789), channel_id=1, source_target_pairs={{0,1},{1,2},{2,3},{3,4},{4,5},{5,6},{6,7},{7,0},{8,9},{9,10},{10,1... | collective-permute-start | bytes 4616 | tf_op jit(solution)/shard_map/while/body/eval_jaxpr/ppermute | solution.py:19
  229.7 3.4 collective-permute-start
  229.7 3.5 collective-permute-start.1
  232.1 5.4 %copy-start.1 = (f32[8,8,4,128]{3,0,2,1:T(8,128)}, f32[8,8,4,128]{3,0,2,1:T(8,128)S(1)}, u32[]{:S(2)}) copy-start(f32[8,8,4,128]{3,0,2,1:T(8,128)S(1)} %fusion.175) | copy-start | bytes 393220 | tf_op jit(solution)/shard_map/while
  233.3 8.8 %collective-permute-start.2 = (f32[8,8,6,1]{3,0,2,1:T(8,128)S(1)}, f32[8,8,6,1]{3,0,2,1:T(8,128)S(1)}, u32[]{:S(2)}, u32[]{:S(2)}) collective-permute-start(f32[8,8,6,1]{3,0,2,1:T(8,128)S(1)} %get-tuple-element.788), channel_id=1, source_target_pairs={{1,0},{2,1},{3,2},{4,3},{5,4},{6,5},{7,6},{0,7},{9,8},{10,9},{11,1... | collective-permute-start | bytes 4616 | tf_op jit(solution)/shard_map/while/body/eval_jaxpr/ppermute | solution.py:20
  237.3 9.8 %collective-permute-start.3 = (f32[8,8,6,1]{3,0,2,1:T(8,128)S(1)}, f32[8,8,6,1]{3,0,2,1:T(8,128)S(1)}, u32[]{:S(2)}, u32[]{:S(2)}) collective-permute-start(f32[8,8,6,1]{3,0,2,1:T(8,128)S(1)} %get-tuple-element.789), channel_id=1, source_target_pairs={{0,1},{1,2},{2,3},{3,4},{4,5},{5,6},{6,7},{7,0},{8,9},{9,10},{10,1... | collective-permute-start | bytes 4616 | tf_op jit(solution)/shard_map/while/body/eval_jaxpr/ppermute | solution.py:19
  297.6 3.4 collective-permute-start
  297.7 3.5 collective-permute-start.1
  300.0 5.4 %copy-start.1 = (f32[8,8,4,128]{3,0,2,1:T(8,128)}, f32[8,8,4,128]{3,0,2,1:T(8,128)S(1)}, u32[]{:S(2)}) copy-start(f32[8,8,4,128]{3,0,2,1:T(8,128)S(1)} %fusion.175) | copy-start | bytes 393220 | tf_op jit(solution)/shard_map/while
  301.3 8.8 %collective-permute-start.2 = (f32[8,8,6,1]{3,0,2,1:T(8,128)S(1)}, f32[8,8,6,1]{3,0,2,1:T(8,128)S(1)}, u32[]{:S(2)}, u32[]{:S(2)}) collective-permute-start(f32[8,8,6,1]{3,0,2,1:T(8,128)S(1)} %get-tuple-element.788), channel_id=1, source_target_pairs={{1,0},{2,1},{3,2},{4,3},{5,4},{6,5},{7,6},{0,7},{9,8},{10,9},{11,1... | collective-permute-start | bytes 4616 | tf_op jit(solution)/shard_map/while/body/eval_jaxpr/ppermute | solution.py:20
  305.2 9.8 %collective-permute-start.3 = (f32[8,8,6,1]{3,0,2,1:T(8,128)S(1)}, f32[8,8,6,1]{3,0,2,1:T(8,128)S(1)}, u32[]{:S(2)}, u32[]{:S(2)}) collective-permute-start(f32[8,8,6,1]{3,0,2,1:T(8,128)S(1)} %get-tuple-element.789), channel_id=1, source_target_pairs={{0,1},{1,2},{2,3},{3,4},{4,5},{5,6},{6,7},{7,0},{8,9},{9,10},{10,1... | collective-permute-start | bytes 4616 | tf_op jit(solution)/shard_map/while/body/eval_jaxpr/ppermute | solution.py:19
  (18 other events, 16.1 us)
where the time goes:
time: 410 us; the launch traced here: 408 us
  blocking collectives  236 us (58%)
  waiting for transfers between devices  61.2 us (15%)
  matrix products  36.9 us (9%)
  starting transfers between devices  35.6 us (9%)
  local copies, waits for them, and re-layouts  15.6 us (4%)
  other arithmetic  13.3 us (3%)
  loops' own time  7.86 us (2%)
    psum x5, blocking collectives, advance(): lax.psum((local, local_total(pending * image), local_total(pending * pend...  196 us
    psum x1, blocking collectives, norm_scale(): squares = lax.psum(local_total(vector * vector), ('gx', 'gy'))  40.3 us
    ppermute x12, waiting for transfers between devices, extended(): before = lax.ppermute(last, axis, up)  34.7 us
    ppermute x12, starting transfers between devices, extended(): after = lax.ppermute(leading, axis, down)  32.4 us
    ppermute x12, waiting for transfers between devices, extended(): after = lax.ppermute(leading, axis, down)  26.5 us
    dot_general x5, matrix products, products(): per_cell = jnp.einsum('kqxy,qxy->kxy', basis, image, precision=highest)  13 us
    reduce_sum x12, other arithmetic, local_total(): return jnp.sum(jnp.sum(values, axis=0))  8.74 us
  transfers between devices with their start and end apart: 24, of which 23 were waited for; matrix products, arithmetic and copies ran while one was open for 1% of the time, Pallas kernels for 0%

commit v1 on v0

--- a/solution.py
+++ b/solution.py
@@ -71,7 +71,9 @@
 
 
 def norm_scale(vector, total):
-    squares = lax.psum(local_total(vector * vector), ("gx", "gy"))
+    part = local_total(vector * vector)
+    pieces = lax.all_gather(part, ("gx", "gy"))
+    squares = jnp.sum(pieces, axis=0)
     return jnp.sqrt(squares / total + FLOOR)
 
 

time: 410 us -> 410 us (level)
    psum x1 -> x0, blocking collectives: 40.3 us -> none  [norm_scale(): squares = lax.psum(local_total(vector * vector), ('gx', 'gy'))]
    unnamed x0 -> x1, blocking collectives: none -> 40.1 us
where the time goes in v1:
time: 410 us; the launch traced here: 409 us
  blocking collectives  236 us (58%)
  waiting for transfers between devices  61.1 us (15%)
  matrix products  36.9 us (9%)
  starting transfers between devices  35.7 us (9%)
  local copies, waits for them, and re-layouts  16.4 us (4%)
  other arithmetic  13.6 us (3%)
  loops' own time  7.87 us (2%)
    psum x5, blocking collectives, advance(): lax.psum((local, local_total(pending * image), local_total(pending * pend...  196 us
    unnamed x1, blocking collectives  40.1 us
    ppermute x12, waiting for transfers between devices, extended(): before = lax.ppermute(last, axis, up)  34.6 us
    ppermute x12, starting transfers between devices, extended(): after = lax.ppermute(leading, axis, down)  32.4 us
    ppermute x12, waiting for transfers between devices, extended(): after = lax.ppermute(leading, axis, down)  26.5 us
    dot_general x5, matrix products, products(): per_cell = jnp.einsum('kqxy,qxy->kxy', basis, image, precision=highest)  13 us
    reduce_sum x12, other arithmetic, local_total(): return jnp.sum(jnp.sum(values, axis=0))  8.45 us
  transfers between devices with their start and end apart: 24, of which 23 were waited for; matrix products, arithmetic and copies ran while one was open for 1% of the time, Pallas kernels for 0%

profile of v1, /device:TPU:0, one launch (start us, length us, event | category | flops | bytes accessed | tf_op | source)
XLA Modules:
  0.0 408.9 jit_solution(10659868201419584903)
XLA Ops:
  2.2 2.0 collective-permute-start.5
  6.0 2.2 collective-permute-start.6
  8.2 3.1 collective-permute-start.7
  12.3 4.8 %collective-permute-done.6 = f32[8,8,6,1]{3,0,2,1:T(8,128)S(1)} collective-permute-done((f32[8,8,6,1]{3,0,2,1:T(8,128)S(1)}, f32[8,8,6,1]{3,0,2,1:T(8,128)S(1)}, u32[]{:S(2)}, u32[]{:S(2)}) %collective-permute-start.6) | collective-permute-done | bytes 1568 | tf_op jit(solution)/shard_map/ppermute | solution.py:19
  17.1 2.8 collective-permute-done.7
  25.9 339.2 %while.31 = (s32[]{:T(128)}, f32[6,64,4,128]{3,2,1,0:T(4,128)S(1)}, f32[6,5]{1,0:T(8,128)S(1)}, f32[64,4,128]{2,1,0:T(4,128)S(1)}, f32[64,4,128]{2,0,1:T(8,128)S...) while((s32[]{:T(128)}, f32[6,64,4,128]{3,2,1,0:T(4,128)S(1)}, ...), condition=%wide.region_6.7_spmd.clone.clone, body=%wide.region_0.6_spmd.clone.clone.sunk | while | flops 14006069 | bytes 9489035 | solution.py:123
  29.6 2.8 collective-permute-start.2
  32.7 4.3 %collective-permute-done.2 = f32[8,8,6,1]{3,0,2,1:T(8,128)S(1)} collective-permute-done((f32[8,8,6,1]{3,0,2,1:T(8,128)S(1)}, f32[8,8,6,1]{3,0,2,1:T(8,128)S(1)}, u32[]{:S(2)}, u32[]{:S(2)}) %collective-permute-start.2) | collective-permute-done | bytes 1568 | tf_op jit(solution)/shard_map/while/body/eval_jaxpr/ppermute | solution.py:20
  37.0 5.2 %collective-permute-done.3 = f32[8,8,6,1]{3,0,2,1:T(8,128)S(1)} collective-permute-done((f32[8,8,6,1]{3,0,2,1:T(8,128)S(1)}, f32[8,8,6,1]{3,0,2,1:T(8,128)S(1)}, u32[]{:S(2)}, u32[]{:S(2)}) %collective-permute-start.3) | collective-permute-done | bytes 1568 | tf_op jit(solution)/shard_map/while/body/eval_jaxpr/ppermute | solution.py:19
  47.2 2.6 convolution_bitcast_fusion.2
  49.8 39.3 %all-reduce.3 = (f32[]{:T(128)}, f32[6]{0:T(128)S(1)}, f32[]{:T(128)}) all-reduce(f32[]{:T(128)} %get-tuple-element.835, f32[6]{0:T(128)S(1)} %convolution_bitcast_fusion.2, f32[]{:T(128)} %fusion.189), channel_id=1, replica_groups=mesh['gx'=4,'gy'=8] {'gx','gy'}, use_global_device_ids=true, to_apply=%region_2.2 | all-reduce | flops 8 | bytes 64 | tf_op jit(solution)/shard_map/while/body/eval_jaxpr/psum | solution.py:110
  96.7 3.9 collective-permute-start.2
  100.9 4.9 %collective-permute-done.2 = f32[8,8,6,1]{3,0,2,1:T(8,128)S(1)} collective-permute-done((f32[8,8,6,1]{3,0,2,1:T(8,128)S(1)}, f32[8,8,6,1]{3,0,2,1:T(8,128)S(1)}, u32[]{:S(2)}, u32[]{:S(2)}) %collective-permute-start.2) | collective-permute-done | bytes 1568 | tf_op jit(solution)/shard_map/while/body/eval_jaxpr/ppermute | solution.py:20
  105.8 5.0 %collective-permute-done.3 = f32[8,8,6,1]{3,0,2,1:T(8,128)S(1)} collective-permute-done((f32[8,8,6,1]{3,0,2,1:T(8,128)S(1)}, f32[8,8,6,1]{3,0,2,1:T(8,128)S(1)}, u32[]{:S(2)}, u32[]{:S(2)}) %collective-permute-start.3) | collective-permute-done | bytes 1568 | tf_op jit(solution)/shard_map/while/body/eval_jaxpr/ppermute | solution.py:19
  115.9 2.6 convolution_bitcast_fusion.2
  118.5 39.2 %all-reduce.3 = (f32[]{:T(128)}, f32[6]{0:T(128)S(1)}, f32[]{:T(128)}) all-reduce(f32[]{:T(128)} %get-tuple-element.835, f32[6]{0:T(128)S(1)} %convolution_bitcast_fusion.2, f32[]{:T(128)} %fusion.189), channel_id=1, replica_groups=mesh['gx'=4,'gy'=8] {'gx','gy'}, use_global_device_ids=true, to_apply=%region_2.2 | all-reduce | flops 8 | bytes 64 | tf_op jit(solution)/shard_map/while/body/eval_jaxpr/psum | solution.py:110
  165.2 3.9 collective-permute-start.2
  169.4 4.6 %collective-permute-done.2 = f32[8,8,6,1]{3,0,2,1:T(8,128)S(1)} collective-permute-done((f32[8,8,6,1]{3,0,2,1:T(8,128)S(1)}, f32[8,8,6,1]{3,0,2,1:T(8,128)S(1)}, u32[]{:S(2)}, u32[]{:S(2)}) %collective-permute-start.2) | collective-permute-done | bytes 1568 | tf_op jit(solution)/shard_map/while/body/eval_jaxpr/ppermute | solution.py:20
  174.0 4.9 %collective-permute-done.3 = f32[8,8,6,1]{3,0,2,1:T(8,128)S(1)} collective-permute-done((f32[8,8,6,1]{3,0,2,1:T(8,128)S(1)}, f32[8,8,6,1]{3,0,2,1:T(8,128)S(1)}, u32[]{:S(2)}, u32[]{:S(2)}) %collective-permute-start.3) | collective-permute-done | bytes 1568 | tf_op jit(solution)/shard_map/while/body/eval_jaxpr/ppermute | solution.py:19
  183.9 2.6 convolution_bitcast_fusion.2
  186.5 39.0 %all-reduce.3 = (f32[]{:T(128)}, f32[6]{0:T(128)S(1)}, f32[]{:T(128)}) all-reduce(f32[]{:T(128)} %get-tuple-element.835, f32[6]{0:T(128)S(1)} %convolution_bitcast_fusion.2, f32[]{:T(128)} %fusion.189), channel_id=1, replica_groups=mesh['gx'=4,'gy'=8] {'gx','gy'}, use_global_device_ids=true, to_apply=%region_2.2 | all-reduce | flops 8 | bytes 64 | tf_op jit(solution)/shard_map/while/body/eval_jaxpr/psum | solution.py:110
  233.1 3.9 collective-permute-start.2
  237.3 4.6 %collective-permute-done.2 = f32[8,8,6,1]{3,0,2,1:T(8,128)S(1)} collective-permute-done((f32[8,8,6,1]{3,0,2,1:T(8,128)S(1)}, f32[8,8,6,1]{3,0,2,1:T(8,128)S(1)}, u32[]{:S(2)}, u32[]{:S(2)}) %collective-permute-start.2) | collective-permute-done | bytes 1568 | tf_op jit(solution)/shard_map/while/body/eval_jaxpr/ppermute | solution.py:20
  241.9 4.9 %collective-permute-done.3 = f32[8,8,6,1]{3,0,2,1:T(8,128)S(1)} collective-permute-done((f32[8,8,6,1]{3,0,2,1:T(8,128)S(1)}, f32[8,8,6,1]{3,0,2,1:T(8,128)S(1)}, u32[]{:S(2)}, u32[]{:S(2)}) %collective-permute-start.3) | collective-permute-done | bytes 1568 | tf_op jit(solution)/shard_map/while/body/eval_jaxpr/ppermute | solution.py:19
  251.8 2.6 convolution_bitcast_fusion.2
  254.4 39.0 %all-reduce.3 = (f32[]{:T(128)}, f32[6]{0:T(128)S(1)}, f32[]{:T(128)}) all-reduce(f32[]{:T(128)} %get-tuple-element.835, f32[6]{0:T(128)S(1)} %convolution_bitcast_fusion.2, f32[]{:T(128)} %fusion.189), channel_id=1, replica_groups=mesh['gx'=4,'gy'=8] {'gx','gy'}, use_global_device_ids=true, to_apply=%region_2.2 | all-reduce | flops 8 | bytes 64 | tf_op jit(solution)/shard_map/while/body/eval_jaxpr/psum | solution.py:110
  301.0 3.9 collective-permute-start.2
  305.2 4.6 %collective-permute-done.2 = f32[8,8,6,1]{3,0,2,1:T(8,128)S(1)} collective-permute-done((f32[8,8,6,1]{3,0,2,1:T(8,128)S(1)}, f32[8,8,6,1]{3,0,2,1:T(8,128)S(1)}, u32[]{:S(2)}, u32[]{:S(2)}) %collective-permute-start.2) | collective-permute-done | bytes 1568 | tf_op jit(solution)/shard_map/while/body/eval_jaxpr/ppermute | solution.py:20
  309.8 4.9 %collective-permute-done.3 = f32[8,8,6,1]{3,0,2,1:T(8,128)S(1)} collective-permute-done((f32[8,8,6,1]{3,0,2,1:T(8,128)S(1)}, f32[8,8,6,1]{3,0,2,1:T(8,128)S(1)}, u32[]{:S(2)}, u32[]{:S(2)}) %collective-permute-start.3) | collective-permute-done | bytes 1568 | tf_op jit(solution)/shard_map/while/body/eval_jaxpr/ppermute | solution.py:19
  319.7 2.6 convolution_bitcast_fusion.2
  322.3 39.0 %all-reduce.3 = (f32[]{:T(128)}, f32[6]{0:T(128)S(1)}, f32[]{:T(128)}) all-reduce(f32[]{:T(128)} %get-tuple-element.835, f32[6]{0:T(128)S(1)} %convolution_bitcast_fusion.2, f32[]{:T(128)} %fusion.189), channel_id=1, replica_groups=mesh['gx'=4,'gy'=8] {'gx','gy'}, use_global_device_ids=true, to_apply=%region_2.2 | all-reduce | flops 8 | bytes 64 | tf_op jit(solution)/shard_map/while/body/eval_jaxpr/psum | solution.py:110
  366.6 40.1 %all-reduce = f32[32]{0:T(128)S(1)} all-reduce(f32[32]{0:T(128)S(1)} %dynamic-update-slice.59), channel_id=1, replica_groups=mesh['gx'=4,'gy'=8] {'gx','gy'}, use_global_device_ids=true, to_apply=%add | all-reduce | flops 32 | bytes 256
  (325 shorter events, 69.3 us)
Async XLA Ops:
  1.5 2.7 copy-start.5
  1.6 4.1 collective-permute-start.4
  2.2 2.3 copy-start.7
  2.2 3.7 collective-permute-start.5
  5.5 6.7 %copy-start.3 = (f32[8,8,4,128]{3,0,2,1:T(8,128)}, f32[8,8,4,128]{3,0,2,1:T(8,128)S(1)}, u32[]{:S(2)}) copy-start(f32[8,8,4,128]{3,0,2,1:T(8,128)S(1)} %fusion.62) | copy-start | bytes 393220
  6.0 11.1 %collective-permute-start.6 = (f32[8,8,6,1]{3,0,2,1:T(8,128)S(1)}, f32[8,8,6,1]{3,0,2,1:T(8,128)S(1)}, u32[]{:S(2)}, u32[]{:S(2)}) collective-permute-start(f32[8,8,6,1]{3,0,2,1:T(8,128)S(1)} %get-tuple-element.682), channel_id=1, source_target_pairs={{0,1},{1,2},{2,3},{3,4},{4,5},{5,6},{6,7},{7,0},{8,9},{9,10},{10,1... | collective-permute-start | bytes 4616 | tf_op jit(solution)/shard_map/ppermute | solution.py:19
  8.2 11.6 %collective-permute-start.7 = (f32[8,8,6,1]{3,0,2,1:T(8,128)S(1)}, f32[8,8,6,1]{3,0,2,1:T(8,128)S(1)}, u32[]{:S(2)}, u32[]{:S(2)}) collective-permute-start(f32[8,8,6,1]{3,0,2,1:T(8,128)S(1)} %get-tuple-element.683), channel_id=1, source_target_pairs={{1,0},{2,1},{3,2},{4,3},{5,4},{6,5},{7,6},{0,7},{9,8},{10,9},{11,1... | collective-permute-start | bytes 4616 | tf_op jit(solution)/shard_map/ppermute | solution.py:20
  26.0 3.4 collective-permute-start
  26.3 3.2 collective-permute-start.1
  28.4 4.2 %copy-start.1 = (f32[8,8,4,128]{3,0,2,1:T(8,128)}, f32[8,8,4,128]{3,0,2,1:T(8,128)S(1)}, u32[]{:S(2)}) copy-start(f32[8,8,4,128]{3,0,2,1:T(8,128)S(1)} %fusion.175) | copy-start | bytes 393220 | tf_op jit(solution)/shard_map/while
  29.6 7.4 %collective-permute-start.2 = (f32[8,8,6,1]{3,0,2,1:T(8,128)S(1)}, f32[8,8,6,1]{3,0,2,1:T(8,128)S(1)}, u32[]{:S(2)}, u32[]{:S(2)}) collective-permute-start(f32[8,8,6,1]{3,0,2,1:T(8,128)S(1)} %get-tuple-element.788), channel_id=1, source_target_pairs={{1,0},{2,1},{3,2},{4,3},{5,4},{6,5},{7,6},{0,7},{9,8},{10,9},{11,1... | collective-permute-start | bytes 4616 | tf_op jit(solution)/shard_map/while/body/eval_jaxpr/ppermute | solution.py:20
  32.4 9.8 %collective-permute-start.3 = (f32[8,8,6,1]{3,0,2,1:T(8,128)S(1)}, f32[8,8,6,1]{3,0,2,1:T(8,128)S(1)}, u32[]{:S(2)}, u32[]{:S(2)}) collective-permute-start(f32[8,8,6,1]{3,0,2,1:T(8,128)S(1)} %get-tuple-element.789), channel_id=1, source_target_pairs={{0,1},{1,2},{2,3},{3,4},{4,5},{5,6},{6,7},{7,0},{8,9},{9,10},{10,1... | collective-permute-start | bytes 4616 | tf_op jit(solution)/shard_map/while/body/eval_jaxpr/ppermute | solution.py:19
  93.0 3.4 collective-permute-start
  93.1 3.5 collective-permute-start.1
  95.4 5.4 %copy-start.1 = (f32[8,8,4,128]{3,0,2,1:T(8,128)}, f32[8,8,4,128]{3,0,2,1:T(8,128)S(1)}, u32[]{:S(2)}) copy-start(f32[8,8,4,128]{3,0,2,1:T(8,128)S(1)} %fusion.175) | copy-start | bytes 393220 | tf_op jit(solution)/shard_map/while
  96.7 9.2 %collective-permute-start.2 = (f32[8,8,6,1]{3,0,2,1:T(8,128)S(1)}, f32[8,8,6,1]{3,0,2,1:T(8,128)S(1)}, u32[]{:S(2)}, u32[]{:S(2)}) collective-permute-start(f32[8,8,6,1]{3,0,2,1:T(8,128)S(1)} %get-tuple-element.788), channel_id=1, source_target_pairs={{1,0},{2,1},{3,2},{4,3},{5,4},{6,5},{7,6},{0,7},{9,8},{10,9},{11,1... | collective-permute-start | bytes 4616 | tf_op jit(solution)/shard_map/while/body/eval_jaxpr/ppermute | solution.py:20
  100.6 10.3 %collective-permute-start.3 = (f32[8,8,6,1]{3,0,2,1:T(8,128)S(1)}, f32[8,8,6,1]{3,0,2,1:T(8,128)S(1)}, u32[]{:S(2)}, u32[]{:S(2)}) collective-permute-start(f32[8,8,6,1]{3,0,2,1:T(8,128)S(1)} %get-tuple-element.789), channel_id=1, source_target_pairs={{0,1},{1,2},{2,3},{3,4},{4,5},{5,6},{6,7},{7,0},{8,9},{9,10},{10,1... | collective-permute-start | bytes 4616 | tf_op jit(solution)/shard_map/while/body/eval_jaxpr/ppermute | solution.py:19
  161.5 3.4 collective-permute-start
  161.6 3.5 collective-permute-start.1
  164.0 5.4 %copy-start.1 = (f32[8,8,4,128]{3,0,2,1:T(8,128)}, f32[8,8,4,128]{3,0,2,1:T(8,128)S(1)}, u32[]{:S(2)}) copy-start(f32[8,8,4,128]{3,0,2,1:T(8,128)S(1)} %fusion.175) | copy-start | bytes 393220 | tf_op jit(solution)/shard_map/while
  165.2 8.8 %collective-permute-start.2 = (f32[8,8,6,1]{3,0,2,1:T(8,128)S(1)}, f32[8,8,6,1]{3,0,2,1:T(8,128)S(1)}, u32[]{:S(2)}, u32[]{:S(2)}) collective-permute-start(f32[8,8,6,1]{3,0,2,1:T(8,128)S(1)} %get-tuple-element.788), channel_id=1, source_target_pairs={{1,0},{2,1},{3,2},{4,3},{5,4},{6,5},{7,6},{0,7},{9,8},{10,9},{11,1... | collective-permute-start | bytes 4616 | tf_op jit(solution)/shard_map/while/body/eval_jaxpr/ppermute | solution.py:20
  169.1 9.8 %collective-permute-start.3 = (f32[8,8,6,1]{3,0,2,1:T(8,128)S(1)}, f32[8,8,6,1]{3,0,2,1:T(8,128)S(1)}, u32[]{:S(2)}, u32[]{:S(2)}) collective-permute-start(f32[8,8,6,1]{3,0,2,1:T(8,128)S(1)} %get-tuple-element.789), channel_id=1, source_target_pairs={{0,1},{1,2},{2,3},{3,4},{4,5},{5,6},{6,7},{7,0},{8,9},{9,10},{10,1... | collective-permute-start | bytes 4616 | tf_op jit(solution)/shard_map/while/body/eval_jaxpr/ppermute | solution.py:19
  229.4 3.4 collective-permute-start
  229.5 3.5 collective-permute-start.1
  231.8 5.4 %copy-start.1 = (f32[8,8,4,128]{3,0,2,1:T(8,128)}, f32[8,8,4,128]{3,0,2,1:T(8,128)S(1)}, u32[]{:S(2)}) copy-start(f32[8,8,4,128]{3,0,2,1:T(8,128)S(1)} %fusion.175) | copy-start | bytes 393220 | tf_op jit(solution)/shard_map/while
  233.1 8.8 %collective-permute-start.2 = (f32[8,8,6,1]{3,0,2,1:T(8,128)S(1)}, f32[8,8,6,1]{3,0,2,1:T(8,128)S(1)}, u32[]{:S(2)}, u32[]{:S(2)}) collective-permute-start(f32[8,8,6,1]{3,0,2,1:T(8,128)S(1)} %get-tuple-element.788), channel_id=1, source_target_pairs={{1,0},{2,1},{3,2},{4,3},{5,4},{6,5},{7,6},{0,7},{9,8},{10,9},{11,1... | collective-permute-start | bytes 4616 | tf_op jit(solution)/shard_map/while/body/eval_jaxpr/ppermute | solution.py:20
  237.0 9.8 %collective-permute-start.3 = (f32[8,8,6,1]{3,0,2,1:T(8,128)S(1)}, f32[8,8,6,1]{3,0,2,1:T(8,128)S(1)}, u32[]{:S(2)}, u32[]{:S(2)}) collective-permute-start(f32[8,8,6,1]{3,0,2,1:T(8,128)S(1)} %get-tuple-element.789), channel_id=1, source_target_pairs={{0,1},{1,2},{2,3},{3,4},{4,5},{5,6},{6,7},{7,0},{8,9},{9,10},{10,1... | collective-permute-start | bytes 4616 | tf_op jit(solution)/shard_map/while/body/eval_jaxpr/ppermute | solution.py:19
  297.3 3.4 collective-permute-start
  297.4 3.5 collective-permute-start.1
  299.7 5.4 %copy-start.1 = (f32[8,8,4,128]{3,0,2,1:T(8,128)}, f32[8,8,4,128]{3,0,2,1:T(8,128)S(1)}, u32[]{:S(2)}) copy-start(f32[8,8,4,128]{3,0,2,1:T(8,128)S(1)} %fusion.175) | copy-start | bytes 393220 | tf_op jit(solution)/shard_map/while
  301.0 8.8 %collective-permute-start.2 = (f32[8,8,6,1]{3,0,2,1:T(8,128)S(1)}, f32[8,8,6,1]{3,0,2,1:T(8,128)S(1)}, u32[]{:S(2)}, u32[]{:S(2)}) collective-permute-start(f32[8,8,6,1]{3,0,2,1:T(8,128)S(1)} %get-tuple-element.788), channel_id=1, source_target_pairs={{1,0},{2,1},{3,2},{4,3},{5,4},{6,5},{7,6},{0,7},{9,8},{10,9},{11,1... | collective-permute-start | bytes 4616 | tf_op jit(solution)/shard_map/while/body/eval_jaxpr/ppermute | solution.py:20
  304.9 9.8 %collective-permute-start.3 = (f32[8,8,6,1]{3,0,2,1:T(8,128)S(1)}, f32[8,8,6,1]{3,0,2,1:T(8,128)S(1)}, u32[]{:S(2)}, u32[]{:S(2)}) collective-permute-start(f32[8,8,6,1]{3,0,2,1:T(8,128)S(1)} %get-tuple-element.789), channel_id=1, source_target_pairs={{0,1},{1,2},{2,3},{3,4},{4,5},{5,6},{6,7},{7,0},{8,9},{9,10},{10,1... | collective-permute-start | bytes 4616 | tf_op jit(solution)/shard_map/while/body/eval_jaxpr/ppermute | solution.py:19
  (18 other events, 17.3 us)
